TPU v7x, 32 devices: a whole 2x2x4 slice. The times are simulated.
32 devices in a mesh: wide: 2 (over x), context: 4 (over z), tensor: 4 (over y, core).
Axes of the slice: x: 2, y: 2, z: 4, core: 2. Of those that a mesh axis runs over, the one named last changes fastest.
Arguments:
- layer_input: bfloat16 [96, 197, 768], P(('wide', 'tensor')), may hold values from -6 to 6
- qkv_weight: bfloat16 [768, 3, 768], P(('wide', 'tensor'), None, 'context'), may hold values from -0.21875 to 0.21875
- proj_weight: bfloat16 [768, 768], P('context', ('wide', 'tensor')), may hold values from -0.875 to 0.875
- norm_gains: bfloat16 [2, 768], P(None, ('wide', 'tensor')), may hold values from 0.5 to 1.5
- norm_biases: bfloat16 [2, 768], P(None, ('wide', 'tensor')), may hold values from -1.796875 to 1.796875
- router_keys: bfloat16 [768, 8], P(('wide', 'tensor')), may hold values from -0.21875 to 0.21875
- up_weight: bfloat16 [8, 768, 3072], P(('wide', 'context'), None, 'tensor'), may hold values from -0.4375 to 0.4375
- down_weight: bfloat16 [8, 3072, 768], P(('wide', 'context'), 'tensor'), may hold values from -0.4375 to 0.4375
- out_cotangent: bfloat16 [96, 197, 768], P(('wide', 'tensor')), may hold values from -6 to 6
Outputs:
- layer_output: bfloat16 [96, 197, 768], P(('wide', 'tensor'))
- rms_stats: float32 [96, 3], P(('wide', 'tensor'))
- input_grad: bfloat16 [96, 197, 768], P(('wide', 'tensor'))
- qkv_grad: float32 [768, 3, 768], P(('wide', 'tensor'), None, 'context')
- proj_grad: float32 [768, 768], P('context', ('wide', 'tensor'))
- gains_grad: float32 [2, 768], P(None, ('wide', 'tensor'))
- biases_grad: float32 [2, 768], P(None, ('wide', 'tensor'))
- router_grad: float32 [768, 8], P(('wide', 'tensor'))
- up_grad: float32 [8, 768, 3072], P(('wide', 'context'), None, 'tensor')
- down_grad: float32 [8, 3072, 768], P(('wide', 'context'), 'tensor')
All inputs are finite; a program needn't handle non-finite values.
Results may differ from a plain program's by a relative error of at most 0.02.
Values may be sent and summed in bfloat16 or wider, within the bound.
A program may use at most 192 MiB of HBM per device.

v0:
```python
import math
import jax
import jax.numpy as jnp
from jax import lax
from jax.sharding import PartitionSpec as P

HEAD_DIM = 64
norm_eps = 1e-06
highest = lax.Precision.HIGHEST
f32 = jnp.float32
bf16 = jnp.bfloat16


def layer_stats(values):
    center = values - jnp.mean(values, axis=-1, keepdims=True)
    spread = lax.rsqrt(jnp.mean(center * center, axis=-1, keepdims=True) + norm_eps)
    return (center * spread, spread)


def norm_back(upstream, scaled, spread):
    return spread * (
        upstream
        - jnp.mean(upstream, axis=-1, keepdims=True)
        - scaled * jnp.mean(upstream * scaled, axis=-1, keepdims=True)
    )


def root_mean(values):
    return jnp.sqrt(jnp.mean(values * values, axis=(1, 2)))


def dot32(spec, a, b, **kw):
    return jnp.einsum(spec, a, b, preferred_element_type=f32, **kw)


def on_device(
    layer_input,
    qkv_weight,
    proj_weight,
    norm_gains,
    norm_biases,
    router_keys,
    up_weight,
    down_weight,
    out_cotangent,
):
    images, length, width = layer_input.shape
    wide_n = lax.axis_size("wide")
    ctx_n = lax.axis_size("context")
    ten_n = lax.axis_size("tensor")
    share = images // ctx_n
    start = lax.axis_index("context") * share
    slots_n = router_keys.shape[1]
    cols = qkv_weight.shape[2]
    rows = qkv_weight.shape[0]
    heads_b = cols // HEAD_DIM
    logit_scale = 1.6 * math.sqrt(width)
    everyone = ("context", "wide", "tensor")
    plane = ("wide", "tensor")
    pack = jnp.concatenate([qkv_weight.reshape(rows, 3 * cols), proj_weight.T], axis=1)
    weights = lax.all_gather(pack, everyone, axis=0, tiled=True).reshape(ctx_n, width, 4 * cols)
    small = jnp.concatenate([norm_gains, norm_biases, router_keys.T], axis=0)
    small = lax.all_gather(small, plane, axis=1, tiled=True).astype(f32)
    gain_vals, bias_vals, router_vals = (small[0:2], small[2:4], small[4:].T)
    qkv_full = weights[:, :, : 3 * cols]
    proj_t = weights[:, :, 3 * cols :]
    x = lax.dynamic_slice_in_dim(layer_input, start, share, 0).astype(f32)
    g = lax.dynamic_slice_in_dim(out_cotangent, start, share, 0)
    hat1, spread1 = layer_stats(x)
    normed1 = (hat1 * gain_vals[0] + bias_vals[0]).astype(bf16)
    qkv = dot32("bld,cdk->cblk", normed1, qkv_full).astype(bf16)
    qkv = qkv.reshape(ctx_n, share, length, 3, heads_b, HEAD_DIM)
    q, k, v = (qkv[:, :, :, 0], qkv[:, :, :, 1], qkv[:, :, :, 2])
    scores = dot32("cbqhd,cbkhd->cbhqk", q, k) * 0.125
    top = jnp.max(scores, axis=-1, keepdims=True)
    exps = jnp.exp(scores - top)
    probs = exps / jnp.sum(exps, axis=-1, keepdims=True)
    probs_low = probs.astype(bf16)
    heads = dot32("cbhqk,cbkhd->cbqhd", probs_low, v).astype(bf16)
    heads = heads.reshape(ctx_n, share, length, cols)
    attention = dot32("cblh,ceh->ble", heads, proj_t)
    residual = x + attention
    hat2, spread2 = layer_stats(residual)
    second = hat2 * gain_vals[1] + bias_vals[1]
    tokens = second.astype(bf16)
    row_scale = lax.rsqrt(jnp.sum(second * second, axis=-1, keepdims=True) + norm_eps)
    unit = second * row_scale
    col_scale = lax.rsqrt(jnp.sum(router_vals * router_vals, axis=0, keepdims=True) + norm_eps)
    keys_unit = router_vals * col_scale
    logits = logit_scale * jnp.einsum("bld,ds->bls", unit, keys_unit, precision=highest)
    dispatch = jax.nn.softmax(logits, axis=1)
    combine = jax.nn.softmax(logits, axis=2)
    dispatch_low = dispatch.astype(bf16)
    combine_low = combine.astype(bf16)
    slots = dot32("bls,bld->sbd", dispatch_low, tokens).astype(bf16)
    dexp = dot32("bls,bld->sbd", combine_low, g).astype(bf16)
    out = jnp.concatenate([slots, dexp], axis=1)
    got = lax.all_to_all(out, ("wide", "context"), split_axis=0, concat_axis=0, tiled=True)
    got = lax.all_gather(got, "tensor", axis=0, tiled=True)
    n = got.shape[0]
    slot_all = got[:, :share].reshape(n * share, width)
    dexp_all = got[:, share:].reshape(n * share, width)
    up, down = (up_weight[0], down_weight[0])
    hidden = dot32("rd,df->rf", slot_all, up)
    active = jax.nn.gelu(hidden).astype(bf16)
    part_out = dot32("rf,fd->rd", active, down)
    active_grad = dot32("rd,fd->rf", dexp_all, down)
    hidden_grad = jax.vjp(jax.nn.gelu, hidden)[1](active_grad)[0].astype(bf16)
    down_grad = dot32("rf,rd->fd", active, dexp_all)[None]
    up_grad = dot32("rd,rf->df", slot_all, hidden_grad)[None]
    part_slot = dot32("rf,df->rd", hidden_grad, up)
    back = jnp.concatenate(
        [part_out.reshape(n, share, width), part_slot.reshape(n, share, width)], axis=1
    ).astype(bf16)
    back = lax.psum_scatter(back, "tensor", scatter_dimension=0, tiled=True)
    back = lax.all_to_all(back, ("wide", "context"), split_axis=0, concat_axis=0, tiled=True)
    expert_out = back[:, :share]
    dslots = back[:, share:]
    mixture = dot32("bls,sbd->bld", combine_low, expert_out)
    result = residual + mixture
    rms = jnp.stack([root_mean(result), root_mean(attention), root_mean(mixture)], axis=-1)
    layer_output = lax.all_gather(result.astype(bf16), "context", axis=0, tiled=True)
    dcomb = dot32("bld,sbd->bls", g, expert_out)
    ddisp = dot32("bld,sbd->bls", tokens, dslots)
    dtokens = dot32("bls,sbd->bld", dispatch_low, dslots)
    dlogits = combine * (dcomb - jnp.sum(combine * dcomb, axis=2, keepdims=True)) + dispatch * (
        ddisp - jnp.sum(dispatch * ddisp, axis=1, keepdims=True)
    )
    dunit = logit_scale * jnp.einsum("bls,ds->bld", dlogits, keys_unit, precision=highest)
    dkeys = logit_scale * jnp.einsum("bld,bls->ds", unit, dlogits, precision=highest)
    drouter = col_scale * (dkeys - keys_unit * jnp.sum(keys_unit * dkeys, axis=0, keepdims=True))
    dsecond = dtokens + row_scale * (dunit - unit * jnp.sum(unit * dunit, axis=-1, keepdims=True))
    dgain2 = jnp.sum(dsecond * hat2, axis=(0, 1))
    dbias2 = jnp.sum(dsecond, axis=(0, 1))
    dresid = g.astype(f32) + norm_back(dsecond * gain_vals[1], hat2, spread2)
    dattn = dresid.astype(bf16)
    dproj = dot32("ble,cblh->ceh", dattn, heads)
    dheads = dot32("ble,ceh->cblh", dattn, proj_t).astype(bf16)
    dheads = dheads.reshape(ctx_n, share, length, heads_b, HEAD_DIM)
    dprobs = dot32("cbqhd,cbkhd->cbhqk", dheads, v)
    dv = dot32("cbhqk,cbqhd->cbkhd", probs_low, dheads)
    ds = (probs * (dprobs - jnp.sum(probs * dprobs, axis=-1, keepdims=True))).astype(bf16)
    dq = dot32("cbhqk,cbkhd->cbqhd", ds, k) * 0.125
    dk = dot32("cbhqk,cbqhd->cbkhd", ds, q) * 0.125
    dqkv = jnp.stack([dq, dk, dv], axis=3).astype(bf16).reshape(ctx_n, share, length, 3 * cols)
    dqkv_w = dot32("bld,cblk->cdk", normed1, dqkv)
    dnormed1 = dot32("cblk,cdk->bld", dqkv, qkv_full)
    dgain1 = jnp.sum(dnormed1 * hat1, axis=(0, 1))
    dbias1 = jnp.sum(dnormed1, axis=(0, 1))
    dx = (dresid + norm_back(dnormed1 * gain_vals[0], hat1, spread1)).astype(bf16)
    input_grad = lax.all_gather(dx, "context", axis=0, tiled=True)
    rms = lax.all_gather(rms, "context", axis=0, tiled=True)
    dpack = jnp.concatenate([dqkv_w, dproj], axis=2).reshape(ctx_n * width, 4 * cols)
    dpack = lax.psum_scatter(dpack.astype(bf16), everyone, scatter_dimension=0, tiled=True)
    dpack = dpack.astype(f32)
    dsmall = jnp.concatenate([jnp.stack([dgain1, dgain2, dbias1, dbias2], axis=1), drouter], axis=1)
    dsmall = lax.psum(dsmall, "context")
    dsmall = lax.psum_scatter(dsmall, plane, scatter_dimension=0, tiled=True)
    return (
        layer_output,
        rms,
        input_grad,
        dpack[:, : 3 * cols].reshape(rows, 3, cols),
        dpack[:, 3 * cols :].T,
        dsmall[:, 0:2].T,
        dsmall[:, 2:4].T,
        dsmall[:, 4:],
        up_grad,
        down_grad,
    )


def solution(mesh):
    images = P(("wide", "tensor"), None, None)
    qkv = P(("wide", "tensor"), None, "context")
    proj = P("context", ("wide", "tensor"))
    lane = P(None, ("wide", "tensor"))
    rowed = P(("wide", "tensor"), None)
    up = P(("wide", "context"), None, "tensor")
    down = P(("wide", "context"), "tensor", None)
    return jax.shard_map(
        on_device,
        mesh=mesh,
        in_specs=(images, qkv, proj, lane, lane, rowed, up, down, images),
        out_specs=(images, rowed, images, qkv, proj, lane, lane, rowed, up, down),
        check_vma=False,
    )
```

profile of v0, /device:TPU:0, one launch (start us, length us, event | category | flops | bytes accessed | tf_op | source)
XLA Modules:
  0.0 542.7 jit_solution(13824113739327236245)
XLA Ops:
  7.2 1.2 copy.120
  8.4 0.8 pad_maximum_fusion.2
  9.2 0.8 copy.121
  10.1 0.7 maximum_bitcast_fusion.1
  10.8 10.6 %all-gather = bf16[8,96,12]{1,2,0:T(8,128)(2,1)S(1)} all-gather(bf16[1,96,12]{1,2,0:T(8,128)(2,1)S(1)} %maximum_bitcast_fusion.1), channel_id=1, replica_groups=mesh['wide'=2,'context'=4,'tensor'=4] {'wide','tensor'}, dimensions={0}, use_global_device_ids=true | all-gather | bytes 20736 | tf_op jit(solution)/shard_map/all_gather | solution.py:63
  21.5 1.4 convert_reduce_fusion
  23.1 1.6 fusion.25
  24.8 53.0 %all-gather.6.cloned.1.call-done = bf16[3072,768]{1,0:T(8,128)(2,1)} async-done(((bf16[96,768]{1,0:T(8,128)(2,1)}), bf16[3072,768]{1,0:T(8,128)(2,1)}) %all-gather.6.cloned.1.call-update) | async-done | bytes 4718608 | tf_op jit(solution)/shard_map/all_gather | solution.py:61
  77.8 6.6 %convert_bitcast_fusion = bf16[4,3,197,576]{3,2,1,0:T(8,128)(2,1)} fusion(bf16[4,768,768]{2,1,0:T(8,128)(2,1)} %bitcast.228, f32[768]{0:T(1024)S(1)} %get-tuple-element.62, f32[768]{0:T(1024)S(1)} %get-tuple-element.63, f32[3,197]{1,0:T(4,128)S(1)} %add_rsqrt_fusion.2, f32[3,197]{1,0:T(4,128)S(1)} %broadcast_multiply_fusion.5, ...), kind=kOutput, calls=%fused_computation.16 | convolution fusion | flops 2095600896 | bytes 7587964 | tf_op jit(solution)/shard_map/bld,cdk->cblk/dot_general | solution.py:33
  84.4 5.8 %copy.124 = bf16[4,3,197,576]{2,3,1,0:T(8,128)(2,1)} copy(bf16[4,3,197,576]{3,2,1,0:T(8,128)(2,1)} %convert_bitcast_fusion) | data formatting | bytes 5446656 | tf_op jit(solution)/shard_map/convert_element_type | solution.py:71
  90.2 2.8 fusion.84
  93.0 6.5 %fusion.140 = (f32[4,3,3,197]{3,2,1,0:T(4,128)S(1)}, f32[4,3,3,197,197]{3,4,2,1,0:T(8,128)S(1)}) fusion(f32[4,3,3,197,197]{3,4,2,1,0:T(8,128)S(1)} %fusion.84), kind=kOutput, calls=%fused_computation.195 | output fusion | flops 5588692 | bytes 11205360 | tf_op jit(solution)/shard_map/sub | solution.py:76
  99.5 3.0 fusion.36
  102.6 4.7 fusion.137
  108.3 2.0 fusion.74
  110.3 0.7 fusion.142
  111.7 1.4 fusion.69
  113.2 10.8 %all_to_all.10 = bf16[8,6,768]{2,1,0:T(8,128)(2,1)S(1)} all-to-all(bf16[8,6,768]{2,1,0:T(8,128)(2,1)S(1)} %copy.130), channel_id=1, replica_groups=mesh['wide'=2,'context'=4,'tensor'=4] {'wide','context'}, dimensions={0} | all-to-all | bytes 147456 | tf_op jit(solution)/shard_map/all_to_all | solution.py:98
  124.1 16.1 %all_gather.20 = bf16[32,6,768]{2,0,1:T(8,128)(2,1)S(1)} all-gather(bf16[8,6,768]{2,0,1:T(8,128)(2,1)S(1)} %copy.131), channel_id=1, replica_groups=mesh['wide'=2,'context'=4,'tensor'=4] {'tensor'}, dimensions={0}, use_global_device_ids=true | all-gather | bytes 368640 | tf_op jit(solution)/shard_map/all_gather | solution.py:99
  141.1 1.0 copy.134
  142.2 0.8 reshape.164
  143.3 2.6 fusion.106
  145.9 1.7 dot_general.96
  147.6 2.1 fusion.65
  149.7 1.6 fusion.62
  151.4 0.7 copy.172
  152.2 16.8 %reduce-scatter.10.cloned.1.call-done = bf16[8,4608]{1,0:T(8,128)(2,1)} async-done(((bf16[32,4608]{1,0:T(8,128)(2,1)}), bf16[8,4608]{1,0:T(8,128)(2,1)}) %reduce-scatter.10.cloned.1.call-update) | async-done | bytes 73744
  169.0 0.9 copy.136
  169.9 12.6 %all_to_all.11 = bf16[8,6,768]{2,1,0:T(8,128)(2,1)S(1)} all-to-all(bf16[8,6,768]{2,1,0:T(8,128)(2,1)S(1)} %copy.136), channel_id=1, replica_groups=mesh['wide'=2,'context'=4,'tensor'=4] {'wide','context'}, dimensions={0} | all-to-all | bytes 147456 | tf_op jit(solution)/shard_map/all_to_all | solution.py:116
  182.5 1.6 multiply_reduce_fusion.11
  184.8 2.2 fusion.119
  187.0 2.9 fusion.122
  189.9 1.8 fusion.114
  191.7 1.7 fusion.117
  193.4 11.0 %multiply_reduce_fusion.2 = (f32[768]{0:T(1024)}, f32[3,197]{1,0:T(4,128)S(1)}, f32[3,197]{1,0:T(4,128)S(1)}, f32[768]{0:T(1024)}, f32[3]{0:T(128)}, /*index=5*/...) fusion(f32[3,197,768]{2,1,0:T(8,128)S(1)} %get-tuple-element.65, f32[3,197]{1,0:T(4,128)S(1)} %copy-done.18, ...), kind=kOutput, calls=%fused_computation.44 | output fusion | flops 13615274 | bytes 10009668 | tf_op jit(solution)/shard_map/mul | solution.py:132
  204.4 2.0 multiply_add_fusion
  206.5 4.0 convolution_convert_fusion
  210.6 5.2 multiply_reduce_fusion
  215.8 4.8 multiply_convert_fusion
  220.6 2.1 fusion.47
  222.8 2.7 fusion.48
  225.5 1.3 fusion.50
  226.8 0.8 pad_maximum_fusion.1
  228.4 7.0 %fusion.24 = (f32[768]{0:T(1024)S(1)}, f32[3,197]{1,0:T(4,128)S(1)}, f32[3,197]{1,0:T(4,128)S(1)}, f32[768]{0:T(1024)S(1)}, f32[3,197,768,1]{2,1,0,3:T(8,128)}) fusion(f32[3,197]{1,0:T(4,128)S(1)} %copy-done.26, f32[3,197]{1,0:T(4,128)S(1)} %copy-done.16, bf16[12,197,768]{2,1,0:T(8,128)(2,1)} %param.9, s32[]{:T(128)S(6)} %select_n.4, ...), kind=kOutput, calls=%fused_computation.38 | convolution fusion | flops 2096051968 | bytes 10217596 | tf_op jit(solution)/shard_map/cblk,cdk->bld/dot_general | solution.py:33
  235.7 0.9 copy.163
  236.8 3.3 fusion.23
  240.8 2.6 fusion.49
  243.4 5.1 fusion.8
  248.4 2.5 pad_maximum_fusion
  250.9 6.6 %copy.147 = bf16[4,768,768]{2,1,0:T(8,128)(2,1)} copy(bf16[4,768,768]{1,2,0:T(8,128)(2,1)} %pad_maximum_fusion) | data formatting | bytes 9437184 | tf_op jit(solution)/shard_map/concatenate | solution.py:153
  258.5 1.9 convolution_bitcast_fusion.1
  260.4 1.9 convolution_bitcast_fusion
  262.4 11.9 %all-gather.1 = f32[4,3,3]{2,1,0:T(4,128)S(1)} all-gather(f32[1,3,3]{2,1,0:T(4,128)S(1)} %bitcast.226), channel_id=1, replica_groups=mesh['wide'=2,'context'=4,'tensor'=4] {'context'}, dimensions={0}, use_global_device_ids=true | all-gather | bytes 180 | tf_op jit(solution)/shard_map/all_gather | solution.py:152
  275.1 0.9 copy.164
  276.0 9.0 %psum.8 = f32[96,12]{0,1:T(8,128)S(1)} all-reduce(f32[96,12]{0,1:T(8,128)S(1)} %copy.164), channel_id=1, replica_groups=mesh['wide'=2,'context'=4,'tensor'=4] {'context'}, use_global_device_ids=true, to_apply=%region_30.0 | all-reduce | flops 1152 | bytes 9216 | tf_op jit(solution)/shard_map/psum | solution.py:157
  286.1 55.5 %all-gather.10.cloned.1.call-done = bf16[12,197,768]{2,1,0:T(8,128)(2,1)} async-done(((bf16[3,197,768]{2,1,0:T(8,128)(2,1)}), bf16[12,197,768]{2,1,0:T(8,128)(2,1)}) %all-gather.10.cloned.1.call-update) | async-done | bytes 3631120 | tf_op jit(solution)/shard_map/all_gather | solution.py:151
  341.6 72.3 %all-gather.8.cloned.1.call-done = bf16[12,197,768]{2,1,0:T(8,128)(2,1)} async-done(((bf16[3,197,768]{2,1,0:T(8,128)(2,1)}), bf16[12,197,768]{2,1,0:T(8,128)(2,1)}) %all-gather.8.cloned.1.call-update) | async-done | bytes 3631120 | tf_op jit(solution)/shard_map/all_gather | solution.py:122
  414.0 111.4 %reduce-scatter.8.cloned.1.call-done = bf16[96,768]{1,0:T(8,128)(2,1)} async-done(((bf16[3072,768]{1,0:T(8,128)(2,1)}), bf16[96,768]{1,0:T(8,128)(2,1)}) %reduce-scatter.8.cloned.1.call-update) | async-done | bytes 147472 | tf_op jit(solution)/shard_map/reduce_scatter | solution.py:154
  525.4 0.9 slice.98
  526.5 0.9 copy.149
  527.3 0.9 convert_element_type.111
  528.4 0.7 copy.150
  529.1 4.3 copy.192
  533.4 1.8 copy.193
  (155 shorter events, 9.5 us)
Async XLA Ops:
  7.2 135.8 %copy-start = (bf16[1,768,768]{2,1,0:T(8,128)(2,1)S(1)}, bf16[1,768,768]{2,1,0:T(8,128)(2,1)}, u32[]{:S(2)}) copy-start(bf16[1,768,768]{2,1,0:T(8,128)(2,1)} %param.15) | copy-start | bytes 3538948
  7.2 70.6 %all-gather.6.cloned.1.call-start = ((), (), s32[]{:S(2)}) async-start(), calls=%async_computation.5 | async-start | bytes 4866048 | tf_op jit(solution)/shard_map/all_gather | solution.py:61
  10.1 159.0 %reduce-scatter.10.cloned.1.call-start = ((), (), s32[]{:S(2)}) async-start(), calls=%async_computation.9 | async-start | bytes 368640
  23.1 61.3 %copy-start.21 = (f32[768]{0:T(1024)}, f32[768]{0:T(1024)S(1)}, u32[]{:S(2)}) copy-start(f32[768]{0:T(1024)S(1)} %get-tuple-element.63) | copy-start | bytes 9220
  23.1 61.3 %copy-start.30 = (f32[768]{0:T(1024)}, f32[768]{0:T(1024)S(1)}, u32[]{:S(2)}) copy-start(f32[768]{0:T(1024)S(1)} %get-tuple-element.62) | copy-start | bytes 9220
  23.1 88.1 %copy-start.23 = (f32[768]{0:T(1024)}, f32[768]{0:T(1024)S(1)}, u32[]{:S(2)}) copy-start(f32[768]{0:T(1024)S(1)} %get-tuple-element.61) | copy-start | bytes 9220
  23.1 61.3 %copy-start.15 = (f32[3,197]{1,0:T(4,128)}, f32[3,197]{1,0:T(4,128)S(1)}, u32[]{:S(2)}) copy-start(f32[3,197]{1,0:T(4,128)S(1)} %broadcast_multiply_fusion.5) | copy-start | bytes 7096
  24.8 83.5 %copy-start.27 = (f32[8]{0:T(128)}, f32[8]{0:T(128)S(1)}, u32[]{:S(2)}) copy-start(f32[8]{0:T(128)S(1)} %add_rsqrt_fusion.3) | copy-start | bytes 100
  24.8 59.6 %copy-start.25 = (f32[3,197]{1,0:T(4,128)}, f32[3,197]{1,0:T(4,128)S(1)}, u32[]{:S(2)}) copy-start(f32[3,197]{1,0:T(4,128)S(1)} %add_rsqrt_fusion.2) | copy-start | bytes 7096
  99.5 3.0 copy-start.2
  99.5 3.0 copy-start.12
  102.6 4.8 copy-start.39
  107.7 3.5 copy-start.17
  108.3 2.0 copy-start.34
  111.0 0.7 copy-start.19
  149.6 1.7 copy-start.9
  151.3 32.8 %copy-start.14 = (f32[3,197,8]{1,2,0:T(8,128)S(1)}, f32[3,197,8]{1,2,0:T(8,128)}, u32[]{:S(2)}) copy-start(f32[3,197,8]{1,2,0:T(8,128)} %get-tuple-element.79) | copy-start | bytes 56740
  151.4 32.8 %copy-start.18 = (f32[3,197]{1,0:T(4,128)S(1)}, f32[3,197]{1,0:T(4,128)}, u32[]{:S(2)}) copy-start(f32[3,197]{1,0:T(4,128)} %copy-done.17) | copy-start | bytes 7096
  151.4 32.8 %copy-start.20 = (f32[3,8]{1,0:T(4,128)S(1)}, f32[3,8]{1,0:T(4,128)}, u32[]{:S(2)}) copy-start(f32[3,8]{1,0:T(4,128)} %copy-done.19) | copy-start | bytes 292
  151.4 32.8 %copy-start.24 = (f32[768]{0:T(1024)S(1)}, f32[768]{0:T(1024)}, u32[]{:S(2)}) copy-start(f32[768]{0:T(1024)} %copy-done.23) | copy-start | bytes 9220
  152.2 122.9 %reduce-scatter.12.cloned.1.call-start = ((), (), s32[]{:S(2)}) async-start(), calls=%async_computation.10 | async-start | bytes 442368
  182.5 2.3 copy-start.28
  182.5 2.4 copy-start.35
  204.4 6.1 %slice-start = ((s8[7372800]{0:T(1024)(128)(4,1)}), s8[4194304]{0:T(1024)(128)(4,1)S(1)}, s32[]{:S(2)}) async-start(s8[7372800]{0:T(1024)(128)(4,1)} %bitcast.205), calls=%async_computation.11 | async-start | bytes 8388608
  206.4 4.1 copy-start.4
  206.4 4.1 slice-start.1
  206.4 4.2 copy-start.3
  206.5 4.1 copy-start.13
  210.5 5.3 copy-start.40
  222.7 2.8 copy-start.41
  222.8 5.4 %slice-start.2 = ((s8[4718592]{0:T(1024)(128)(4,1)}), s8[4194304]{0:T(1024)(128)(4,1)S(1)}, s32[]{:S(2)}) async-start(s8[4718592]{0:T(1024)(128)(4,1)} %bitcast.231), calls=%async_computation.13 | async-start | bytes 8388608
  225.5 2.7 slice-start.3
  227.7 0.7 copy-start.16
  227.7 0.7 copy-start.22
  227.7 0.7 copy-start.26
  228.2 7.3 %copy-start.7 = (bf16[4,3,197,3,3,64]{2,5,4,3,1,0:T(8,128)(2,1)}, bf16[4,3,197,3,3,64]{2,5,4,3,1,0:T(8,128)(2,1)S(1)}, u32[]{:S(2)}) copy-start(bf16[4,3,197,3,3,64]{2,5,4,3,1,0:T(8,128)(2,1)S(1)} %copy.144) | copy-start | bytes 8169988
  228.4 7.1 %copy-start.33 = (f32[768]{0:T(1024)S(1)}, f32[768]{0:T(1024)}, u32[]{:S(2)}) copy-start(f32[768]{0:T(1024)} %get-tuple-element.52) | copy-start | bytes 9220
  228.4 7.1 %copy-start.32 = (f32[768]{0:T(1024)S(1)}, f32[768]{0:T(1024)}, u32[]{:S(2)}) copy-start(f32[768]{0:T(1024)} %get-tuple-element.56) | copy-start | bytes 9220
  228.4 7.1 %copy-start.29 = (f32[8]{0:T(128)S(1)}, f32[8]{0:T(128)}, u32[]{:S(2)}) copy-start(f32[8]{0:T(128)} %copy-done.27) | copy-start | bytes 100
  228.4 7.1 %copy-start.36 = (f32[8]{0:T(128)S(1)}, f32[8]{0:T(128)}, u32[]{:S(2)}) copy-start(f32[8]{0:T(128)} %get-tuple-element.90) | copy-start | bytes 100
  228.4 8.4 %copy-start.5 = (f32[3,197,768]{2,1,0:T(8,128)S(1)}, f32[3,197,768]{2,1,0:T(8,128)}, u32[]{:S(2)}) copy-start(f32[3,197,768]{2,1,0:T(8,128)} %copy-done.4) | copy-start | bytes 5446660
  236.7 104.9 %all-gather.10.cloned.1.call-start = ((), (), s32[]{:S(2)}) async-start(), calls=%async_computation.7 | async-start | bytes 4608000 | tf_op jit(solution)/shard_map/all_gather | solution.py:151
  240.1 173.8 %all-gather.8.cloned.1.call-start = ((), (), s32[]{:S(2)}) async-start(), calls=%async_computation.6 | async-start | bytes 4608000 | tf_op jit(solution)/shard_map/all_gather | solution.py:122
  240.7 2.6 copy-start.31
  240.7 284.6 %reduce-scatter.8.cloned.1.call-start = ((), (), s32[]{:S(2)}) async-start(), calls=%async_computation.8 | async-start | bytes 4866048 | tf_op jit(solution)/shard_map/reduce_scatter | solution.py:154
  240.8 2.6 copy-start.8
  257.6 0.7 copy-start.42
  257.6 0.9 copy-start.11
  257.6 2.8 copy-start.10
  260.4 1.9 copy-start.37
  260.4 1.9 copy-start.38
  529.1 4.3 copy-start.6
  533.4 2.1 copy-start.1
Sparse Core Ops, SparseCore 0:
  11.5 66.2 all-gather.5
  152.3 16.6 reduce-scatter.9
  236.8 30.2 reduce-scatter.11
  269.1 72.4 all-gather.9
  343.0 70.8 all-gather.7
  419.3 106.0 reduce-scatter.7
where the time goes:
time: 552 us; the launch traced here: 543 us
  waiting for transfers between devices  310 us (56%)
  matrix products  72.2 us (13%)
  blocking collectives  71 us (13%)
  other arithmetic  38.7 us (7%)
  local copies, waits for them, and re-layouts  35.6 us (6%)
  between operations  15.3 us (3%)
    reduce_scatter x1, waiting for transfers between devices, on_device(): lax.psum_scatter(dpack.astype(bf16), everyone, scatter_dimension=0, tiled...  111 us
    all_gather x1, waiting for transfers between devices, on_device(): lax.all_gather(result.astype(bf16), 'context', axis=0, tiled=True)  72.3 us
    dot_general x24, matrix products, dot32(): return jnp.einsum(spec, a, b, preferred_element_type=f32, **kw)  65.1 us
    all_gather x1, waiting for transfers between devices, on_device(): input_grad = lax.all_gather(dx, 'context', axis=0, tiled=True)  55.5 us
    all_gather x1, waiting for transfers between devices, on_device(): lax.all_gather(pack, everyone, axis=0, tiled=True)  53 us
    unnamed x8, waiting for transfers between devices  17.4 us
    all_gather x1, blocking collectives, on_device(): got = lax.all_gather(got, 'tensor', axis=0, tiled=True)  16.1 us
    unnamed x103, local copies, waits for them, and re-layouts  13.7 us
  transfers between devices with their start and end apart: 6, of which 5 were waited for; matrix products, arithmetic and copies ran while one was open for 6% of the time, Pallas kernels for 0%

commit v1 on v0

--- a/solution.py
+++ b/solution.py
@@ -9,6 +9,18 @@
 highest = lax.Precision.HIGHEST
 f32 = jnp.float32
 bf16 = jnp.bfloat16
+
+
+def split_up(value, dim, devices):
+    dims = value.shape
+    blocks = value.reshape(*dims[:dim], devices, dims[dim] // devices, *dims[dim + 1 :])
+    return jnp.moveaxis(blocks, dim, 0)
+
+
+def laid_out(blocks, dim):
+    lengths = list(blocks.shape[1:])
+    lengths[dim] *= blocks.shape[0]
+    return jnp.moveaxis(blocks, 0, dim).reshape(lengths)
 
 
 def layer_stats(values):
@@ -113,7 +125,17 @@
         [part_out.reshape(n, share, width), part_slot.reshape(n, share, width)], axis=1
     ).astype(bf16)
     back = lax.psum_scatter(back, "tensor", scatter_dimension=0, tiled=True)
-    back = lax.all_to_all(back, ("wide", "context"), split_axis=0, concat_axis=0, tiled=True)
+    length_2, index = (lax.axis_size(("wide", "context")), lax.axis_index(("wide", "context")))
+    tiles = split_up(back, 0, length_2)
+    out_2 = tiles
+    for lap in range(1, length_2):
+        target, source = ((index + lap) % length_2, (index - lap) % length_2)
+        sent = lax.dynamic_index_in_dim(tiles, target, 0)
+        other = lax.ppermute(
+            sent, ("wide", "context"), [(i, (i + lap) % length_2) for i in range(length_2)]
+        )
+        out_2 = lax.dynamic_update_slice_in_dim(out_2, other, source, axis=0)
+    back = laid_out(out_2, 0)
     expert_out = back[:, :share]
     dslots = back[:, share:]
     mixture = dot32("bls,sbd->bld", combine_low, expert_out)

time: 552 us -> 561 us (1.016)
  blocking collectives: 71 us -> 50.9 us
  starting transfers between devices: 0.24 us -> 12.6 us
  local copies, waits for them, and re-layouts: 35.6 us -> 47.2 us
  matrix products: 72.2 us -> 78.6 us
    all_to_all x1 -> x0, blocking collectives: 12.6 us -> none  [on_device(): lax.all_to_all(back, ('wide', 'context'), split_axis=0, concat_axis=0, ti...]
    ppermute x0 -> x7, starting transfers between devices: none -> 12.2 us  [on_device(): lax.ppermute(sent, ('wide', 'context'), [(i, (i + lap) % length_2) for i...]
    dynamic_update_slice x0 -> x7, local copies, waits for them, and re-layouts: none -> 11 us  [on_device(): out_2 = lax.dynamic_update_slice_in_dim(out_2, other, source, axis=0)]
    all_gather x1, blocking collectives: 16.1 us -> 6.33 us  [on_device(): got = lax.all_gather(got, 'tensor', axis=0, tiled=True)]
    dot_general x24, matrix products: 65.1 us -> 70.9 us  [dot32(): return jnp.einsum(spec, a, b, preferred_element_type=f32, **kw)]
    unnamed x103 -> x116, local copies, waits for them, and re-layouts: 13.7 us -> 13.8 us
  transfers between devices with their start and end apart: 6 -> 13, of which waited for: 5 -> 8; matrix products, arithmetic and copies ran while one was open for 6% -> 6% of each run, Pallas kernels for 0% -> 0%
where the time goes in v1:
time: 561 us; the launch traced here: 551 us
  waiting for transfers between devices  312 us (56%)
  matrix products  78.6 us (14%)
  blocking collectives  50.9 us (9%)
  local copies, waits for them, and re-layouts  47.2 us (8%)
  other arithmetic  34.7 us (6%)
  between operations  15.3 us (3%)
  starting transfers between devices  12.6 us (2%)
    reduce_scatter x1, waiting for transfers between devices, on_device(): lax.psum_scatter(dpack.astype(bf16), everyone, scatter_dimension=0, tiled...  111 us
    all_gather x1, waiting for transfers between devices, on_device(): lax.all_gather(result.astype(bf16), 'context', axis=0, tiled=True)  72.4 us
    dot_general x24, matrix products, dot32(): return jnp.einsum(spec, a, b, preferred_element_type=f32, **kw)  70.9 us
    all_gather x1, waiting for transfers between devices, on_device(): input_grad = lax.all_gather(dx, 'context', axis=0, tiled=True)  56.4 us
    all_gather x1, waiting for transfers between devices, on_device(): lax.all_gather(pack, everyone, axis=0, tiled=True)  53 us
    unnamed x8, waiting for transfers between devices  17.3 us
    unnamed x116, local copies, waits for them, and re-layouts  13.8 us
    ppermute x7, starting transfers between devices, on_device(): lax.ppermute(sent, ('wide', 'context'), [(i, (i + lap) % length_2) for i...  12.2 us
  transfers between devices with their start and end apart: 13, of which 8 were waited for; matrix products, arithmetic and copies ran while one was open for 6% of the time, Pallas kernels for 0%

profile of v1, /device:TPU:0, one launch (start us, length us, event | category | flops | bytes accessed | tf_op | source)
XLA Modules:
  0.0 551.5 jit_solution(7027963614523241768)
XLA Ops:
  7.2 1.2 copy.149
  10.8 10.6 %all-gather = bf16[8,96,12]{1,2,0:T(8,128)(2,1)S(1)} all-gather(bf16[1,96,12]{1,2,0:T(8,128)(2,1)S(1)} %maximum_bitcast_fusion.1), channel_id=1, replica_groups=mesh['wide'=2,'context'=4,'tensor'=4] {'wide','tensor'}, dimensions={0}, use_global_device_ids=true | all-gather | bytes 20736 | tf_op jit(solution)/shard_map/all_gather | solution.py:75
  21.5 1.4 convert_reduce_fusion
  23.2 1.6 fusion.25
  24.8 53.0 %all-gather.6.cloned.1.call-done = bf16[3072,768]{1,0:T(8,128)(2,1)} async-done(((bf16[96,768]{1,0:T(8,128)(2,1)}), bf16[3072,768]{1,0:T(8,128)(2,1)}) %all-gather.6.cloned.1.call-update) | async-done | bytes 4718608 | tf_op jit(solution)/shard_map/all_gather | solution.py:73
  77.8 6.6 %convert_bitcast_fusion = bf16[4,3,197,576]{3,2,1,0:T(8,128)(2,1)} fusion(bf16[4,768,768]{2,1,0:T(8,128)(2,1)} %bitcast.271, f32[768]{0:T(1024)S(1)} %get-tuple-element.62, f32[768]{0:T(1024)S(1)} %get-tuple-element.63, f32[3,197]{1,0:T(4,128)S(1)} %add_rsqrt_fusion.2, f32[3,197]{1,0:T(4,128)S(1)} %broadcast_multiply_fusion.5, ...), kind=kOutput, calls=%fused_computation.16 | convolution fusion | flops 2095600896 | bytes 7587964 | tf_op jit(solution)/shard_map/bld,cdk->cblk/dot_general | solution.py:45
  84.4 5.8 %copy.153 = bf16[4,3,197,576]{2,3,1,0:T(8,128)(2,1)} copy(bf16[4,3,197,576]{3,2,1,0:T(8,128)(2,1)} %convert_bitcast_fusion) | data formatting | bytes 5446656 | tf_op jit(solution)/shard_map/convert_element_type | solution.py:83
  90.2 2.8 fusion.71
  93.0 6.5 %fusion.125 = (f32[4,3,3,197]{3,2,1,0:T(4,128)S(1)}, f32[4,3,3,197,197]{3,4,2,1,0:T(8,128)S(1)}) fusion(f32[4,3,3,197,197]{3,4,2,1,0:T(8,128)S(1)} %fusion.71), kind=kOutput, calls=%fused_computation.199 | output fusion | flops 5588692 | bytes 11205360 | tf_op jit(solution)/shard_map/sub | solution.py:88
  99.6 3.0 fusion.34
  102.6 4.7 fusion.123
  108.3 2.0 convolution_multiply_fusion
  112.3 1.4 fusion.64
  113.7 10.8 %all_to_all.5 = bf16[8,6,768]{2,1,0:T(8,128)(2,1)S(1)} all-to-all(bf16[8,6,768]{2,1,0:T(8,128)(2,1)S(1)} %copy.159), channel_id=1, replica_groups=mesh['wide'=2,'context'=4,'tensor'=4] {'wide','context'}, dimensions={0} | all-to-all | bytes 147456 | tf_op jit(solution)/shard_map/all_to_all | solution.py:110
  124.6 6.3 %all_gather.20 = bf16[32,6,768]{2,0,1:T(8,128)(2,1)S(1)} all-gather(bf16[8,6,768]{2,0,1:T(8,128)(2,1)S(1)} %copy.160), channel_id=1, replica_groups=mesh['wide'=2,'context'=4,'tensor'=4] {'tensor'}, dimensions={0}, use_global_device_ids=true | all-gather | bytes 368640 | tf_op jit(solution)/shard_map/all_gather | solution.py:111
  131.9 1.0 copy.163
  134.0 2.6 fusion.87
  136.6 1.7 dot_general.96
  138.3 2.1 fusion.60
  140.5 1.6 fusion.57
  143.1 16.7 %reduce-scatter.10.cloned.1.call-done = bf16[8,4608]{1,0:T(8,128)(2,1)} async-done(((bf16[32,4608]{1,0:T(8,128)(2,1)}), bf16[8,4608]{1,0:T(8,128)(2,1)}) %reduce-scatter.10.cloned.1.call-update) | async-done | bytes 73744
  159.7 1.3 constant_dynamic-slice_fusion
  161.1 1.6 collective-permute-start
  162.6 2.4 collective-permute-start.1
  165.0 2.4 collective-permute-start.2
  167.9 1.5 collective-permute-start.4
  169.5 1.5 collective-permute-start.5
  170.9 2.4 collective-permute-start.6
  175.0 1.6 dynamic_update_slice.28
  176.6 1.6 dynamic_update_slice.29
  178.2 1.6 dynamic_update_slice.30
  179.8 1.6 dynamic_update_slice.31
  181.3 1.6 dynamic_update_slice.32
  182.9 1.6 dynamic_update_slice.33
  184.5 1.6 dynamic_update_slice.34
  186.0 1.6 multiply_reduce_fusion.11
  187.6 1.4 multiply_reduce_fusion.10
  189.1 2.7 fusion.100
  191.9 2.9 fusion.103
  194.8 6.0 %fusion = f32[3,197,768]{2,1,0:T(8,128)} fusion(f32[3,197,768]{2,1,0:T(8,128)} %fusion.103, f32[3,197]{1,0:T(4,128)S(1)} %copy-done.24, f32[768]{0:T(1024)S(1)} %copy-done.18, f32[768]{0:T(1024)S(1)} %get-tuple-element.60, f32[3,197]{1,0:T(4,128)S(1)} %add_rsqrt_fusion.1, f32[3,197,768]{2,1,0:T(8,128)S(1)} %get-tuple-element.65, ...), kind=kOutput, calls=%fused_computation | output fusion | flops 3178574 | bytes 5459892 | tf_op jit(solution)/shard_map/mul | solution.py:154
  200.8 4.4 multiply_add_fusion.1
  205.1 4.2 multiply_reduce_fusion.2
  209.3 2.5 multiply_add_fusion
  211.9 4.0 convolution_convert_fusion
  216.0 5.2 multiply_reduce_fusion
  221.2 4.8 multiply_convert_fusion
  226.1 2.1 fusion.42
  228.2 2.7 fusion.43
  230.9 1.3 fusion.45
  233.9 7.0 %fusion.24 = (f32[768]{0:T(1024)S(1)}, f32[3,197]{1,0:T(4,128)S(1)}, f32[3,197]{1,0:T(4,128)S(1)}, f32[768]{0:T(1024)S(1)}, f32[3,197,768,1]{2,1,0,3:T(8,128)}) fusion(f32[3,197]{1,0:T(4,128)S(1)} %copy-done.31, f32[3,197]{1,0:T(4,128)S(1)} %copy-done.22, bf16[12,197,768]{2,1,0:T(8,128)(2,1)} %param.9, s32[]{:T(128)S(6)} %select_n.106, ...), kind=kOutput, calls=%fused_computation.38 | convolution fusion | flops 2096051968 | bytes 10217596 | tf_op jit(solution)/shard_map/cblk,cdk->bld/dot_general | solution.py:45
  242.2 3.3 fusion.23
  246.5 2.5 fusion.44
  249.0 5.1 fusion.8
  254.1 2.5 pad_maximum_fusion
  256.6 6.6 %copy.187 = bf16[4,768,768]{2,1,0:T(8,128)(2,1)} copy(bf16[4,768,768]{1,2,0:T(8,128)(2,1)} %pad_maximum_fusion) | data formatting | bytes 9437184 | tf_op jit(solution)/shard_map/concatenate | solution.py:175
  264.1 1.9 convolution_bitcast_fusion.1
  266.0 1.9 convolution_bitcast_fusion
  268.1 11.9 %all-gather.1 = f32[4,3,3]{2,1,0:T(4,128)S(1)} all-gather(f32[1,3,3]{2,1,0:T(4,128)S(1)} %bitcast.269), channel_id=1, replica_groups=mesh['wide'=2,'context'=4,'tensor'=4] {'context'}, dimensions={0}, use_global_device_ids=true | all-gather | bytes 180 | tf_op jit(solution)/shard_map/all_gather | solution.py:174
  281.6 11.3 %psum.8 = f32[96,12]{0,1:T(8,128)S(1)} all-reduce(f32[96,12]{0,1:T(8,128)S(1)} %copy.204), channel_id=1, replica_groups=mesh['wide'=2,'context'=4,'tensor'=4] {'context'}, use_global_device_ids=true, to_apply=%region_30.31 | all-reduce | flops 1152 | bytes 9216 | tf_op jit(solution)/shard_map/psum | solution.py:179
  294.1 56.4 %all-gather.10.cloned.1.call-done = bf16[12,197,768]{2,1,0:T(8,128)(2,1)} async-done(((bf16[3,197,768]{2,1,0:T(8,128)(2,1)}), bf16[12,197,768]{2,1,0:T(8,128)(2,1)}) %all-gather.10.cloned.1.call-update) | async-done | bytes 3631120 | tf_op jit(solution)/shard_map/all_gather | solution.py:173
  350.5 72.4 %all-gather.8.cloned.1.call-done = bf16[12,197,768]{2,1,0:T(8,128)(2,1)} async-done(((bf16[3,197,768]{2,1,0:T(8,128)(2,1)}), bf16[12,197,768]{2,1,0:T(8,128)(2,1)}) %all-gather.8.cloned.1.call-update) | async-done | bytes 3631120 | tf_op jit(solution)/shard_map/all_gather | solution.py:144
  422.9 111.4 %reduce-scatter.8.cloned.1.call-done = bf16[96,768]{1,0:T(8,128)(2,1)} async-done(((bf16[3072,768]{1,0:T(8,128)(2,1)}), bf16[96,768]{1,0:T(8,128)(2,1)}) %reduce-scatter.8.cloned.1.call-update) | async-done | bytes 147472 | tf_op jit(solution)/shard_map/reduce_scatter | solution.py:176
  538.0 4.3 copy.246
  542.3 1.8 copy.247
  (194 shorter events, 22.6 us)
Async XLA Ops:
  7.2 126.5 %copy-start = (bf16[1,768,768]{2,1,0:T(8,128)(2,1)S(1)}, bf16[1,768,768]{2,1,0:T(8,128)(2,1)}, u32[]{:S(2)}) copy-start(bf16[1,768,768]{2,1,0:T(8,128)(2,1)} %param.15) | copy-start | bytes 3538948
  7.2 70.6 %all-gather.6.cloned.1.call-start = ((), (), s32[]{:S(2)}) async-start(), calls=%async_computation.4 | async-start | bytes 4866048 | tf_op jit(solution)/shard_map/all_gather | solution.py:73
  10.1 149.7 %reduce-scatter.10.cloned.1.call-start = ((), (), s32[]{:S(2)}) async-start(), calls=%async_computation.8 | async-start | bytes 368640
  23.1 61.3 %copy-start.28 = (f32[768]{0:T(1024)}, f32[768]{0:T(1024)S(1)}, u32[]{:S(2)}) copy-start(f32[768]{0:T(1024)S(1)} %get-tuple-element.63) | copy-start | bytes 9220
  23.1 61.3 %copy-start.35 = (f32[768]{0:T(1024)}, f32[768]{0:T(1024)S(1)}, u32[]{:S(2)}) copy-start(f32[768]{0:T(1024)S(1)} %get-tuple-element.62) | copy-start | bytes 9220
  23.1 88.6 %copy-start.17 = (f32[768]{0:T(1024)}, f32[768]{0:T(1024)S(1)}, u32[]{:S(2)}) copy-start(f32[768]{0:T(1024)S(1)} %get-tuple-element.61) | copy-start | bytes 9220
  23.1 61.3 %copy-start.21 = (f32[3,197]{1,0:T(4,128)}, f32[3,197]{1,0:T(4,128)S(1)}, u32[]{:S(2)}) copy-start(f32[3,197]{1,0:T(4,128)S(1)} %broadcast_multiply_fusion.5) | copy-start | bytes 7096
  24.8 83.5 %copy-start.32 = (f32[8]{0:T(128)}, f32[8]{0:T(128)S(1)}, u32[]{:S(2)}) copy-start(f32[8]{0:T(128)S(1)} %add_rsqrt_fusion.3) | copy-start | bytes 100
  24.8 59.6 %copy-start.30 = (f32[3,197]{1,0:T(4,128)}, f32[3,197]{1,0:T(4,128)S(1)}, u32[]{:S(2)}) copy-start(f32[3,197]{1,0:T(4,128)S(1)} %add_rsqrt_fusion.2) | copy-start | bytes 7096
  99.5 3.0 copy-start.2
  99.5 3.0 copy-start.14
  102.6 4.8 copy-start.42
  108.3 2.0 copy-start.23
  111.1 1.1 copy-start.26
  111.7 0.6 copy-start.19
  140.4 1.7 copy-start.9
  140.4 45.6 %copy-start.13 = (f32[3,197,8]{1,2,0:T(8,128)S(1)}, f32[3,197,8]{1,2,0:T(8,128)}, u32[]{:S(2)}) copy-start(f32[3,197,8]{1,2,0:T(8,128)} %get-tuple-element.82) | copy-start | bytes 56740
  140.5 45.6 %copy-start.20 = (f32[3,197]{1,0:T(4,128)S(1)}, f32[3,197]{1,0:T(4,128)}, u32[]{:S(2)}) copy-start(f32[3,197]{1,0:T(4,128)} %copy-done.19) | copy-start | bytes 7096
  142.1 45.5 %copy-start.16 = (f32[3,197,8]{1,2,0:T(8,128)S(1)}, f32[3,197,8]{1,2,0:T(8,128)}, u32[]{:S(2)}) copy-start(f32[3,197,8]{1,2,0:T(8,128)} %get-tuple-element.84) | copy-start | bytes 56740
  142.1 45.5 %copy-start.18 = (f32[768]{0:T(1024)S(1)}, f32[768]{0:T(1024)}, u32[]{:S(2)}) copy-start(f32[768]{0:T(1024)} %copy-done.17) | copy-start | bytes 9220
  142.1 45.5 %copy-start.27 = (f32[3,8]{1,0:T(4,128)S(1)}, f32[3,8]{1,0:T(4,128)}, u32[]{:S(2)}) copy-start(f32[3,8]{1,0:T(4,128)} %copy-done.26) | copy-start | bytes 292
  142.9 137.9 %reduce-scatter.12.cloned.1.call-start = ((), (), s32[]{:S(2)}) async-start(), calls=%async_computation.9 | async-start | bytes 442368
  161.1 8.4 %collective-permute-start = (bf16[1,1,6,768]{3,2,1,0:T(8,128)(2,1)S(1)}, bf16[1,1,6,768]{3,2,1,0:T(8,128)(2,1)S(1)}, u32[]{:S(2)}, u32[]{:S(2)}) collective-permute-start(bf16[1,1,6,768]{3,2,1,0:T(8,128)(2,1)S(1)} %bitcast.268), channel_id=1, source_target_pairs={{0,4},{4,8},{8,12},{12,16},{16,20},{20,24},{24,28},{28,0},{1,5},{5... | collective-permute-start | bytes 27656 | tf_op jit(solution)/shard_map/ppermute | solution.py:134
  162.6 8.3 %collective-permute-start.1 = (bf16[1,1,6,768]{3,2,1,0:T(8,128)(2,1)S(1)}, bf16[1,1,6,768]{3,2,1,0:T(8,128)(2,1)S(1)}, u32[]{:S(2)}, u32[]{:S(2)}) collective-permute-start(bf16[1,1,6,768]{3,2,1,0:T(8,128)(2,1)S(1)} %bitcast.267), channel_id=1, source_target_pairs={{0,8},{4,12},{8,16},{12,20},{16,24},{20,28},{24,0},{28,4},{1,9},{5... | collective-permute-start | bytes 27656 | tf_op jit(solution)/shard_map/ppermute | solution.py:134
  165.0 8.3 %collective-permute-start.2 = (bf16[1,1,6,768]{3,2,1,0:T(8,128)(2,1)S(1)}, bf16[1,1,6,768]{3,2,1,0:T(8,128)(2,1)S(1)}, u32[]{:S(2)}, u32[]{:S(2)}) collective-permute-start(bf16[1,1,6,768]{3,2,1,0:T(8,128)(2,1)S(1)} %bitcast.258), channel_id=1, source_target_pairs={{0,12},{4,16},{8,20},{12,24},{16,28},{20,0},{24,4},{28,8},{1,13},{... | collective-permute-start | bytes 27656 | tf_op jit(solution)/shard_map/ppermute | solution.py:134
  167.4 6.0 %collective-permute-start.3 = (bf16[1,1,6,768]{3,2,1,0:T(8,128)(2,1)S(1)}, bf16[1,1,6,768]{3,2,1,0:T(8,128)(2,1)S(1)}, u32[]{:S(2)}, u32[]{:S(2)}) collective-permute-start(bf16[1,1,6,768]{3,2,1,0:T(8,128)(2,1)S(1)} %bitcast.260), channel_id=1, source_target_pairs={{0,16},{4,20},{8,24},{12,28},{16,0},{20,4},{24,8},{28,12},{1,17},{... | collective-permute-start | bytes 27656 | tf_op jit(solution)/shard_map/ppermute | solution.py:134
  167.9 5.5 collective-permute-start.4
  169.5 4.7 collective-permute-start.5
  170.9 4.1 collective-permute-start.6
  175.0 14.1 %copy-start.24 = (f32[3,197]{1,0:T(4,128)S(1)}, f32[3,197]{1,0:T(4,128)}, u32[]{:S(2)}) copy-start(f32[3,197]{1,0:T(4,128)} %copy-done.23) | copy-start | bytes 7096
  175.0 14.1 %copy-start.33 = (f32[8]{0:T(128)S(1)}, f32[8]{0:T(128)}, u32[]{:S(2)}) copy-start(f32[8]{0:T(128)} %copy-done.32) | copy-start | bytes 100
  194.8 6.0 %copy-start.12 = (bf16[8,6,768]{2,0,1:T(8,128)(2,1)S(1)}, bf16[8,6,768]{2,0,1:T(8,128)(2,1)}, u32[]{:S(2)}) copy-start(bf16[8,6,768]{2,0,1:T(8,128)(2,1)} %dynamic_update_slice.34) | copy-start | bytes 221188
  209.3 6.7 %slice-start = ((s8[7372800]{0:T(1024)(128)(4,1)}), s8[4194304]{0:T(1024)(128)(4,1)S(1)}, s32[]{:S(2)}) async-start(s8[7372800]{0:T(1024)(128)(4,1)} %bitcast.233), calls=%async_computation.10 | async-start | bytes 8388608
  211.8 4.1 copy-start.4
  211.8 4.1 slice-start.1
  211.9 4.2 copy-start.3
  211.9 4.2 copy-start.15
  215.9 5.3 copy-start.43
  228.2 2.8 copy-start.44
  228.2 5.4 slice-start.2
  230.9 2.7 slice-start.3
  233.1 0.7 copy-start.22
  233.1 0.7 copy-start.29
  233.1 0.7 copy-start.31
  233.6 7.3 %copy-start.7 = (bf16[4,3,197,3,3,64]{2,5,4,3,1,0:T(8,128)(2,1)}, bf16[4,3,197,3,3,64]{2,5,4,3,1,0:T(8,128)(2,1)S(1)}, u32[]{:S(2)}) copy-start(bf16[4,3,197,3,3,64]{2,5,4,3,1,0:T(8,128)(2,1)S(1)} %copy.184) | copy-start | bytes 8169988
  233.8 7.1 %copy-start.38 = (f32[768]{0:T(1024)S(1)}, f32[768]{0:T(1024)}, u32[]{:S(2)}) copy-start(f32[768]{0:T(1024)} %get-tuple-element.52) | copy-start | bytes 9220
  233.8 7.1 %copy-start.37 = (f32[768]{0:T(1024)S(1)}, f32[768]{0:T(1024)}, u32[]{:S(2)}) copy-start(f32[768]{0:T(1024)} %get-tuple-element.56) | copy-start | bytes 9220
  233.8 7.1 %copy-start.25 = (f32[768,8]{0,1:T(8,128)S(1)}, f32[768,8]{0,1:T(8,128)}, u32[]{:S(2)}) copy-start(f32[768,8]{0,1:T(8,128)} %get-tuple-element.95) | copy-start | bytes 73732
  233.8 7.1 %copy-start.34 = (f32[8]{0:T(128)S(1)}, f32[8]{0:T(128)}, u32[]{:S(2)}) copy-start(f32[8]{0:T(128)} %copy-done.32) | copy-start | bytes 100
  233.8 7.1 %copy-start.39 = (f32[8]{0:T(128)S(1)}, f32[8]{0:T(128)}, u32[]{:S(2)}) copy-start(f32[8]{0:T(128)} %get-tuple-element.94) | copy-start | bytes 100
  233.8 8.4 %copy-start.5 = (f32[3,197,768]{2,1,0:T(8,128)S(1)}, f32[3,197,768]{2,1,0:T(8,128)}, u32[]{:S(2)}) copy-start(f32[3,197,768]{2,1,0:T(8,128)} %copy-done.4) | copy-start | bytes 5446660
  242.1 108.4 %all-gather.10.cloned.1.call-start = ((), (), s32[]{:S(2)}) async-start(), calls=%async_computation.6 | async-start | bytes 4608000 | tf_op jit(solution)/shard_map/all_gather | solution.py:173
  245.6 177.3 %all-gather.8.cloned.1.call-start = ((), (), s32[]{:S(2)}) async-start(), calls=%async_computation.5 | async-start | bytes 4608000 | tf_op jit(solution)/shard_map/all_gather | solution.py:144
  246.2 2.8 copy-start.36
  246.2 288.1 %reduce-scatter.8.cloned.1.call-start = ((), (), s32[]{:S(2)}) async-start(), calls=%async_computation.7 | async-start | bytes 4866048 | tf_op jit(solution)/shard_map/reduce_scatter | solution.py:176
  246.4 2.6 copy-start.8
  263.2 0.7 copy-start.45
  263.2 0.9 copy-start.11
  263.2 2.8 copy-start.10
  266.0 1.9 copy-start.40
  266.0 1.9 copy-start.41
  538.0 4.3 copy-start.6
  542.3 2.1 copy-start.1
Sparse Core Ops, SparseCore 0:
  11.5 66.2 all-gather.5
  143.0 16.6 reduce-scatter.9
  242.3 34.2 reduce-scatter.11
  278.0 72.4 all-gather.9
  351.9 70.9 all-gather.7
  428.2 106.0 reduce-scatter.7
